TPU v7x, 32 devices: a whole 2x2x4 slice. The times are simulated.
32 devices in a mesh: row: 4 (over y, x), col: 8 (over z, core).
Axes of the slice: x: 2, y: 2, z: 4, core: 2. Of those that a mesh axis runs over, the one named last changes fastest.
Arguments:
- charge: float32 [256, 256, 256], P('col', 'row'), may hold values from -6 to 6
- green_spectrum: float32 [512, 512, 512], P('row', 'col'), may hold values from 0.2 to 2
Outputs:
- potential: float32 [256, 256, 256], P('col', 'row')
All inputs are finite; a program needn't handle non-finite values.
Results may differ from a plain program's by a relative error of at most 0.00007.
Values sent between devices are 32-bit elements; how exact they have to be, the bound alone decides.
A program may use at most 192 MiB of HBM per device.

v0:
```python
import math
import jax
import jax.numpy as jnp
from jax import lax
from jax.sharding import PartitionSpec as P

M = 512
N = 256


def phases(count_in, count_out, length):
    row_ids = lax.iota(jnp.int32, count_in)[:, None]
    col_ids = lax.iota(jnp.int32, count_out)[None, :]
    turn_ids = row_ids * col_ids % length
    angles = turn_ids.astype(jnp.float32) * (2.0 * math.pi / length)
    return (jnp.cos(angles), jnp.sin(angles))


def forward_table(count_in, count_out, length):
    cosine, sine_part = phases(count_in, count_out, length)
    return jnp.stack([jnp.stack([cosine, -sine_part], 1), jnp.stack([sine_part, cosine], 1)], 0)


def inverse_table(count_in, count_out, length):
    cosine, sine_part = phases(count_in, count_out, length)
    scaling = 1.0 / length
    return (
        jnp.stack([jnp.stack([cosine, sine_part], 1), jnp.stack([-sine_part, cosine], 1)], 0)
        * scaling
    )


def contract(pattern, left_side, right_side):
    return jnp.einsum(
        pattern,
        left_side,
        right_side,
        precision=lax.Precision.HIGHEST,
        preferred_element_type=jnp.float32,
    )


def on_device(charge, green_spectrum):
    cosine, sine_part = phases(N, M, M)
    real_table = jnp.stack([cosine, -sine_part], 1)
    along_z = contract("xyz,zqk->xyqk", charge, real_table)
    by_rows = lax.all_to_all(along_z, "row", split_axis=3, concat_axis=1, tiled=True)
    forward = forward_table(N, M, M)
    along_y = contract("xypk,pyqb->xkqb", by_rows, forward)
    spectrum = contract(
        "xkpj,pxqa->kjqa",
        lax.all_to_all(along_y, "col", split_axis=3, concat_axis=0, tiled=True),
        forward,
    )
    product = spectrum * green_spectrum[:, :, None, :]
    back_table = inverse_table(M, N, M)
    back_cos, back_sin = phases(M, N, M)
    real_back = jnp.stack([back_cos, -back_sin], 0) * (1.0 / M)
    back_x = contract("kjqa,qapx->kjpx", product, back_table)
    by_cols = lax.all_to_all(back_x, "col", split_axis=3, concat_axis=1, tiled=True)
    back_y = contract("kbpx,pbqy->kxqy", by_cols, back_table)
    return contract(
        "cxpy,pcz->xyz",
        lax.all_to_all(back_y, "row", split_axis=3, concat_axis=0, tiled=True),
        real_back,
    )


def solution(mesh):
    in_specs = (P("col", "row", None), P("row", "col", None))
    out_specs = P("col", "row", None)
    return jax.shard_map(
        on_device, mesh=mesh, in_specs=in_specs, out_specs=out_specs, check_vma=False
    )
```

profile of v0, /device:TPU:0, one launch (start us, length us, event | category | flops | bytes accessed | tf_op | source)
XLA Modules:
  0.0 1348.2 jit_solution(13706535293127981104)
XLA Ops:
  2.1 9.0 convolution_bitcast_fusion.1
  11.1 16.2 %copy.38 = f32[32,64,2,512]{1,0,2,3:T(8,128)} copy(f32[32,64,2,512]{3,1,0,2:T(8,128)} %convolution_bitcast_fusion.1) | data formatting | bytes 16777216 | tf_op jit(solution)/shard_map/xyz,zqk->xyqk/dot_general | solution.py:34
  27.3 14.3 %reshape.237 = f32[4,1,524288]{2,1,0:T(1,128)} reshape(f32[512,2,32,64]{3,2,1,0:T(8,128)} %bitcast.107) | data formatting | bytes 16777216
  49.7 91.6 %all-to-all-done = f32[4,1,524288]{2,1,0:T(1,128)} async-done(((f32[4,1,524288]{2,1,0:T(1,128)}), f32[4,1,524288]{2,1,0:T(1,128)}, u32[]{:S(2)}, u32[]{:S(2)}) %all-to-all-start) | async-done | bytes 8388640 | tf_op jit(solution)/shard_map/all_to_all | solution.py:47
  141.9 28.2 %reduce = f32[4,524288]{1,0:T(4,128)} reduce(f32[4,1,524288]{2,1,0:T(1,128)} %all-to-all-done, f32[]{:T(128)} %broadcast.343), dimensions={1}, to_apply=%all_to_all.52.reduce_sub_computation | reduce | bytes 16777220 | tf_op jit(solution)/shard_map/all_to_all | solution.py:47
  170.1 16.8 %reshape.238 = f32[512,2,32,64]{3,2,1,0:T(8,128)} reshape(f32[4,524288]{1,0:T(4,128)} %reduce) | data formatting | bytes 16777216
  186.9 12.8 copy.67
  204.3 30.4 %convolution_bitcast_fusion = f32[32,128,2,512]{3,1,2,0:T(8,128)} fusion(f32[32,256,2,128,1]{3,1,2,4,0:T(8,128)S(1)} %bitcast.111, f32[1,256,2,512]{3,1,2,0:T(8,128)S(1)} %get-tuple-element.8, f32[1,256,2,512]{3,1,2,0:T(8,128)S(1)} %get-tuple-element.7), kind=kOutput, calls=%fused_computation.9 | convolution fusion | flops 25770328064 | bytes 27262976 | tf_op jit(solution)/shard_map/xypk,pyqb->xkqb/dot_general | solution.py:34
  234.7 25.1 %copy.43 = f32[32,128,2,512]{1,2,0,3:T(2,128)} copy(f32[32,128,2,512]{3,1,2,0:T(8,128)} %convolution_bitcast_fusion) | data formatting | bytes 33554432 | tf_op jit(solution)/shard_map/xypk,pyqb->xkqb/dot_general | solution.py:34
  259.8 5.9 all-to-all-start.1
  265.7 17.7 %copy.48 = f32[128,64,512]{2,0,1:T(8,128)} copy(f32[128,64,512]{2,1,0:T(8,128)} %param.3) | data formatting | bytes 33554432 | tf_op args[1]
  290.0 339.3 %all-to-all-done.1 = f32[32,128,2,512]{1,2,0,3:T(2,128)} async-done(((f32[32,128,2,512]{1,2,0,3:T(2,128)}), f32[32,128,2,512]{1,2,0,3:T(2,128)}, u32[]{:S(2)}, u32[]{:S(2)}) %all-to-all-start.1) | async-done | bytes 16777248 | tf_op jit(solution)/shard_map/all_to_all | solution.py:52
  629.3 11.0 copy.44
  642.1 71.3 %fusion.4 = f32[128,64,2,512,1]{3,0,4,2,1:T(8,128)} fusion(f32[256,128,2,64,1]{1,3,2,0,4:T(8,128)S(1)} %bitcast.106, f32[2,256,2,512,1]{3,1,0,2,4:T(8,128)S(1)} %copy-done.2), kind=kOutput, calls=%fused_computation.5 | convolution fusion | flops 51539607552 | bytes 52428800 | tf_op jit(solution)/shard_map/xkpj,pxqa->kjqa/dot_general | solution.py:34
  713.5 58.4 %fusion.7 = f32[128,64,2,256]{3,0,2,1:T(8,128)} fusion(f32[128,64,2,512,1]{3,0,4,2,1:T(8,128)} %fusion.4, f32[128,64,512]{2,0,1:T(8,128)} %copy.48, f32[1,512,2,256]{3,1,0,2:T(8,128)S(1)} %copy-done.3, f32[1,512,2,256]{3,1,0,2:T(8,128)S(1)} %get-tuple-element.5), kind=kOutput, calls=%fused_computation.8 | convolution fusion | flops 51549044736 | bytes 69206016 | tf_op jit(solution)/shard_map/kjqa,qapx->kjpx/dot_general | solution.py:34
  771.9 25.0 %copy.50 = f32[128,64,2,256]{0,2,1,3:T(2,128)} copy(f32[128,64,2,256]{3,0,2,1:T(8,128)} %fusion.7) | data formatting | bytes 33554432 | tf_op jit(solution)/shard_map/kjqa,qapx->kjpx/dot_general | solution.py:34
  796.9 367.8 %all_to_all.72 = f32[128,64,2,256]{0,2,1,3:T(2,128)S(1)} all-to-all(f32[128,64,2,256]{0,2,1,3:T(2,128)} %copy.50), channel_id=1, replica_groups=mesh['row'=4,'col'=8] {'col'}, dimensions={3} | all-to-all | bytes 33554432 | tf_op jit(solution)/shard_map/all_to_all | solution.py:60
  1164.7 10.3 copy.51
  1175.0 7.0 copy.52
  1182.0 37.7 %fusion.13 = f32[128,32,2,256]{3,0,2,1:T(8,128)} fusion(f32[128,512,2,32,1]{0,3,2,1,4:T(8,128)} %bitcast.114, f32[1,512,2,256]{3,1,0,2:T(8,128)S(1)} %copy-done.4, f32[1,512,2,256]{3,1,0,2:T(8,128)S(1)} %get-tuple-element.5), kind=kOutput, calls=%fused_computation.13 | convolution fusion | flops 25770852352 | bytes 27262976 | tf_op jit(solution)/shard_map/kbpx,pbqy->kxqy/dot_general | solution.py:34
  1219.6 13.2 copy.54
  1240.8 90.0 %all-to-all-done.3 = f32[128,32,2,256]{0,2,1,3:T(2,128)} async-done(((f32[128,32,2,256]{0,2,1,3:T(2,128)}), f32[128,32,2,256]{0,2,1,3:T(2,128)}, u32[]{:S(2)}, u32[]{:S(2)}) %all-to-all-start.3) | async-done | bytes 8388640 | tf_op jit(solution)/shard_map/all_to_all | solution.py:64
  1330.8 8.4 copy.55
  1339.2 8.5 fusion.22
  (23 shorter events, 31.7 us)
Async XLA Ops:
  0.0 2.1 copy-start
  41.7 99.7 %all-to-all-start = ((f32[4,1,524288]{2,1,0:T(1,128)}), f32[4,1,524288]{2,1,0:T(1,128)}, u32[]{:S(2)}, u32[]{:S(2)}) async-start(f32[4,1,524288]{2,1,0:T(1,128)} %reshape.237), calls=%async_computation | async-start | bytes 16777216 | tf_op jit(solution)/shard_map/all_to_all | solution.py:47
  259.8 369.5 %all-to-all-start.1 = ((f32[32,128,2,512]{1,2,0,3:T(2,128)}), f32[32,128,2,512]{1,2,0,3:T(2,128)}, u32[]{:S(2)}, u32[]{:S(2)}) async-start(f32[32,128,2,512]{1,2,0,3:T(2,128)} %copy.43), calls=%async_computation.1 | async-start | bytes 33554432 | tf_op jit(solution)/shard_map/all_to_all | solution.py:52
  640.3 1.8 copy-start.2
  642.1 71.4 %copy-start.3 = (f32[1,512,2,256]{3,1,0,2:T(8,128)S(1)}, f32[1,512,2,256]{3,1,0,2:T(8,128)}, u32[]{:S(2)}) copy-start(f32[1,512,2,256]{3,1,0,2:T(8,128)} %get-tuple-element.6) | copy-start | bytes 3145732
  1175.0 7.0 copy-start.4
  1232.9 97.9 %all-to-all-start.3 = ((f32[128,32,2,256]{0,2,1,3:T(2,128)}), f32[128,32,2,256]{0,2,1,3:T(2,128)}, u32[]{:S(2)}, u32[]{:S(2)}) async-start(f32[128,32,2,256]{0,2,1,3:T(2,128)} %copy.54), calls=%async_computation.3 | async-start | bytes 16777216 | tf_op jit(solution)/shard_map/all_to_all | solution.py:64
  1330.8 16.9 %copy-start.1 = (f32[32,64,256]{2,1,0:T(8,128)S(1)}, f32[32,64,256]{2,1,0:T(8,128)}, u32[]{:S(2)}) copy-start(f32[32,64,256]{2,1,0:T(8,128)} %param.2) | copy-start | bytes 6291460
where the time goes:
time: 1360 us; the launch traced here: 1350 us
  waiting for transfers between devices  521 us (38%)
  blocking collectives  368 us (27%)
  matrix products  215 us (16%)
  local copies, waits for them, and re-layouts  185 us (14%)
  other arithmetic  41.2 us (3%)
  starting transfers between devices  17.6 us (1%)
    all_to_all x1, blocking collectives, on_device(): lax.all_to_all(back_x, 'col', split_axis=3, concat_axis=1, tiled=True)  368 us
    all_to_all x1, waiting for transfers between devices, on_device(): lax.all_to_all(along_y, 'col', split_axis=3, concat_axis=0, tiled=True)  339 us
    dot_general x6, matrix products, contract(): jnp.einsum(pattern, left_side, right_side, precision=lax.Precision.HIGHES...  215 us
    all_to_all x1, waiting for transfers between devices, on_device(): lax.all_to_all(along_z, 'row', split_axis=3, concat_axis=1, tiled=True)  91.6 us
    all_to_all x1, waiting for transfers between devices, on_device(): lax.all_to_all(back_y, 'row', split_axis=3, concat_axis=0, tiled=True)  90 us
    dot_general x4, local copies, waits for them, and re-layouts, contract(): jnp.einsum(pattern, left_side, right_side, precision=lax.Precision.HIGHES...  79.6 us
    unnamed x13, local copies, waits for them, and re-layouts  48.9 us
    all_to_all x1, other arithmetic, on_device(): lax.all_to_all(along_z, 'row', split_axis=3, concat_axis=1, tiled=True)  28.2 us
  transfers between devices with their start and end apart: 3, of which 3 were waited for; matrix products, arithmetic and copies ran while one was open for 2% of the time, Pallas kernels for 0%

commit v1 on v0

--- a/solution.py
+++ b/solution.py
@@ -6,6 +6,28 @@
 
 M = 512
 N = 256
+
+
+def split_up(value, dim, devices):
+    before, after = (value.shape[:dim], value.shape[dim + 1 :])
+    return jnp.moveaxis(value.reshape(*before, devices, -1, *after), dim, 0)
+
+
+def laid_out(blocks, dim):
+    lengths = list(blocks.shape[1:])
+    lengths[dim] *= blocks.shape[0]
+    return jnp.moveaxis(blocks, 0, dim).reshape(lengths)
+
+
+def swapped_with_each(shard, axis, split_dim, concat_dim):
+    length, index = (lax.axis_size(axis), lax.axis_index(axis))
+    tiles = split_up(shard, split_dim, length)
+    outs = [tiles[index]]
+    for turn in range(1, length):
+        sent = tiles[index ^ turn]
+        outs.append(lax.ppermute(sent, axis, [(i, i ^ turn) for i in range(length)]))
+    tiles = jnp.stack(outs)[index ^ jnp.arange(length)]
+    return laid_out(tiles, concat_dim)
 
 
 def phases(count_in, count_out, length):
@@ -44,7 +66,7 @@
     cosine, sine_part = phases(N, M, M)
     real_table = jnp.stack([cosine, -sine_part], 1)
     along_z = contract("xyz,zqk->xyqk", charge, real_table)
-    by_rows = lax.all_to_all(along_z, "row", split_axis=3, concat_axis=1, tiled=True)
+    by_rows = swapped_with_each(along_z, "row", 3, 1)
     forward = forward_table(N, M, M)
     along_y = contract("xypk,pyqb->xkqb", by_rows, forward)
     spectrum = contract(

time: 1360 us -> 1310 us (0.963)
  other arithmetic: 41.2 us -> 16.6 us
  local copies, waits for them, and re-layouts: 185 us -> 161 us
    all_to_all x1 -> x0, waiting for transfers between devices: 91.6 us -> none  [on_device(): lax.all_to_all(along_z, 'row', split_axis=3, concat_axis=1, tiled=True)]
    ppermute x0 -> x3, waiting for transfers between devices: none -> 87.5 us  [swapped_with_each(): lax.ppermute(sent, axis, [(i, i ^ turn) for i in range(length)])]
    unnamed x13 -> x11, local copies, waits for them, and re-layouts: 48.9 us -> 17.8 us
    all_to_all x1 -> x0, other arithmetic: 28.2 us -> none  [on_device(): lax.all_to_all(along_z, 'row', split_axis=3, concat_axis=1, tiled=True)]
    another operation x0 -> x5, local copies, waits for them, and re-layouts: none -> 19.8 us
    all_to_all x3 -> x0, local copies, waits for them, and re-layouts: 18 us -> none  [on_device(): lax.all_to_all(along_z, 'row', split_axis=3, concat_axis=1, tiled=True)]
    dot_general x4 -> x3, local copies, waits for them, and re-layouts: 79.6 us -> 63.3 us  [contract(): jnp.einsum(pattern, left_side, right_side, precision=lax.Precision.HIGHES...]
  transfers between devices with their start and end apart: 3 -> 5, of which waited for: 3 -> 4; matrix products, arithmetic and copies ran while one was open for 2% -> 2% of each run, Pallas kernels for 0% -> 0%
where the time goes in v1:
time: 1310 us; the launch traced here: 1290 us
  waiting for transfers between devices  517 us (39%)
  blocking collectives  368 us (28%)
  matrix products  216 us (16%)
  local copies, waits for them, and re-layouts  161 us (12%)
  other arithmetic  16.6 us (1%)
  starting transfers between devices  16.5 us (1%)
    all_to_all x1, blocking collectives, on_device(): lax.all_to_all(back_x, 'col', split_axis=3, concat_axis=1, tiled=True)  368 us
    all_to_all x1, waiting for transfers between devices, on_device(): lax.all_to_all(along_y, 'col', split_axis=3, concat_axis=0, tiled=True)  339 us
    dot_general x6, matrix products, contract(): jnp.einsum(pattern, left_side, right_side, precision=lax.Precision.HIGHES...  216 us
    all_to_all x1, waiting for transfers between devices, on_device(): lax.all_to_all(back_y, 'row', split_axis=3, concat_axis=0, tiled=True)  90 us
    ppermute x3, waiting for transfers between devices, swapped_with_each(): lax.ppermute(sent, axis, [(i, i ^ turn) for i in range(length)])  87.5 us
    dot_general x3, local copies, waits for them, and re-layouts, contract(): jnp.einsum(pattern, left_side, right_side, precision=lax.Precision.HIGHES...  63.3 us
  transfers between devices with their start and end apart: 5, of which 4 were waited for; matrix products, arithmetic and copies ran while one was open for 2% of the time, Pallas kernels for 0%

profile of v1, /device:TPU:0, one launch (start us, length us, event | category | flops | bytes accessed | tf_op | source)
XLA Modules:
  0.0 1294.9 jit_solution(15800418459900412227)
XLA Ops:
  2.1 9.0 convolution_bitcast_fusion.1
  11.1 9.9 reshape.251
  21.0 19.2 %constant_dynamic-slice_fusion.3 = (f32[32,64,2,1,128]{4,3,1,0,2:T(1,128)S(1)}, f32[32,64,2,1,128]{4,3,1,0,2:T(1,128)S(1)}, f32[32,64,2,1,128]{4,3,1,0,2:T(1,128)S(1)}, f32[32,64,2,1,128]{4,3,1,0,2:T(1,128)S(1)}) fusion(f32[32,64,2,4,128]{4,3,1,0,2:T(4,128)} %reshape.251, s32[]{:T(128)S(6)} %select_n.97, s32[]{:T(128)S(6)} %select_n.100, s32[]{:T(128)S(6)} %select_n.99, ...), kind=kLoop, calls=%fused_computation.83 | loop fusion | bytes 16777232 | tf_op jit(solution)/shard_map/dynamic-slice
  47.7 43.1 %collective-permute-done.2 = f32[32,64,2,128]{3,1,2,0:T(8,128)S(1)} collective-permute-done((f32[32,64,2,128]{3,1,2,0:T(8,128)S(1)}, f32[32,64,2,128]{3,1,2,0:T(8,128)S(1)}, u32[]{:S(2)}, u32[]{:S(2)}) %collective-permute-start.2) | collective-permute-done | bytes 2097184 | tf_op jit(solution)/shard_map/ppermute | solution.py:28
  90.9 44.3 %collective-permute-done = f32[32,64,2,128]{3,1,2,0:T(8,128)S(1)} collective-permute-done((f32[32,64,2,128]{3,1,2,0:T(8,128)S(1)}, f32[32,64,2,128]{3,1,2,0:T(8,128)S(1)}, u32[]{:S(2)}, u32[]{:S(2)}) %collective-permute-start) | collective-permute-done | bytes 2097184 | tf_op jit(solution)/shard_map/ppermute | solution.py:28
  138.9 7.7 gather_fusion
  150.8 30.5 %convolution_bitcast_fusion = f32[32,128,2,512]{3,1,2,0:T(8,128)} fusion(f32[32,256,2,128,1]{3,1,2,4,0:T(8,128)S(1)} %bitcast.127, f32[1,256,2,512]{3,1,2,0:T(8,128)S(1)} %get-tuple-element.12, f32[1,256,2,512]{3,1,2,0:T(8,128)S(1)} %get-tuple-element.11), kind=kOutput, calls=%fused_computation.10 | convolution fusion | flops 25770328064 | bytes 27262976 | tf_op jit(solution)/shard_map/xypk,pyqb->xkqb/dot_general | solution.py:56
  181.3 25.1 %copy.31 = f32[32,128,2,512]{1,2,0,3:T(2,128)} copy(f32[32,128,2,512]{3,1,2,0:T(8,128)} %convolution_bitcast_fusion) | data formatting | bytes 33554432 | tf_op jit(solution)/shard_map/xypk,pyqb->xkqb/dot_general | solution.py:56
  206.4 5.9 all-to-all-start
  212.3 17.7 %copy.36 = f32[128,64,512]{2,0,1:T(8,128)} copy(f32[128,64,512]{2,1,0:T(8,128)} %param.3) | data formatting | bytes 33554432 | tf_op args[1]
  236.7 339.2 %all-to-all-done = f32[32,128,2,512]{1,2,0,3:T(2,128)} async-done(((f32[32,128,2,512]{1,2,0,3:T(2,128)}), f32[32,128,2,512]{1,2,0,3:T(2,128)}, u32[]{:S(2)}, u32[]{:S(2)}) %all-to-all-start) | async-done | bytes 16777248 | tf_op jit(solution)/shard_map/all_to_all | solution.py:74
  575.9 11.0 copy.32
  588.8 71.4 %fusion.4 = f32[128,64,2,512,1]{3,0,4,2,1:T(8,128)} fusion(f32[256,128,2,64,1]{1,3,2,0,4:T(8,128)S(1)} %bitcast.124, f32[2,256,2,512,1]{3,1,0,2,4:T(8,128)S(1)} %copy-done.2), kind=kOutput, calls=%fused_computation.6 | convolution fusion | flops 51539607552 | bytes 52428800 | tf_op jit(solution)/shard_map/xkpj,pxqa->kjqa/dot_general | solution.py:56
  660.1 58.5 %fusion.7 = f32[128,64,2,256]{3,0,2,1:T(8,128)} fusion(f32[128,64,2,512,1]{3,0,4,2,1:T(8,128)} %fusion.4, f32[128,64,512]{2,0,1:T(8,128)} %copy.36, f32[1,512,2,256]{3,1,0,2:T(8,128)S(1)} %copy-done.3, f32[1,512,2,256]{3,1,0,2:T(8,128)S(1)} %get-tuple-element.9), kind=kOutput, calls=%fused_computation.9 | convolution fusion | flops 51549044736 | bytes 69206016 | tf_op jit(solution)/shard_map/kjqa,qapx->kjpx/dot_general | solution.py:56
  718.6 25.0 %copy.38 = f32[128,64,2,256]{0,2,1,3:T(2,128)} copy(f32[128,64,2,256]{3,0,2,1:T(8,128)} %fusion.7) | data formatting | bytes 33554432 | tf_op jit(solution)/shard_map/kjqa,qapx->kjpx/dot_general | solution.py:56
  743.7 367.8 %all_to_all.54 = f32[128,64,2,256]{0,2,1,3:T(2,128)S(1)} all-to-all(f32[128,64,2,256]{0,2,1,3:T(2,128)} %copy.38), channel_id=1, replica_groups=mesh['row'=4,'col'=8] {'col'}, dimensions={3} | all-to-all | bytes 33554432 | tf_op jit(solution)/shard_map/all_to_all | solution.py:82
  1111.4 10.3 copy.39
  1121.7 7.0 copy.40
  1128.7 37.7 %fusion.13 = f32[128,32,2,256]{3,0,2,1:T(8,128)} fusion(f32[128,512,2,32,1]{0,3,2,1,4:T(8,128)} %bitcast.130, f32[1,512,2,256]{3,1,0,2:T(8,128)S(1)} %copy-done.4, f32[1,512,2,256]{3,1,0,2:T(8,128)S(1)} %get-tuple-element.9), kind=kOutput, calls=%fused_computation.15 | convolution fusion | flops 25770852352 | bytes 27262976 | tf_op jit(solution)/shard_map/kbpx,pbqy->kxqy/dot_general | solution.py:56
  1166.4 13.2 %copy.42 = f32[128,32,2,256]{0,2,1,3:T(2,128)} copy(f32[128,32,2,256]{3,0,2,1:T(8,128)} %fusion.13) | data formatting | bytes 16777216 | tf_op jit(solution)/shard_map/kbpx,pbqy->kxqy/dot_general | solution.py:56
  1179.6 5.9 all-to-all-start.2
  1187.6 90.0 %all-to-all-done.2 = f32[128,32,2,256]{0,2,1,3:T(2,128)} async-done(((f32[128,32,2,256]{0,2,1,3:T(2,128)}), f32[128,32,2,256]{0,2,1,3:T(2,128)}, u32[]{:S(2)}, u32[]{:S(2)}) %all-to-all-start.2) | async-done | bytes 8388640 | tf_op jit(solution)/shard_map/all_to_all | solution.py:86
  1277.5 8.4 copy.43
  1285.9 8.5 fusion.22
  (31 shorter events, 27.9 us)
Async XLA Ops:
  0.0 2.1 copy-start
  40.4 50.5 %collective-permute-start.2 = (f32[32,64,2,128]{3,1,2,0:T(8,128)S(1)}, f32[32,64,2,128]{3,1,2,0:T(8,128)S(1)}, u32[]{:S(2)}, u32[]{:S(2)}) collective-permute-start(f32[32,64,2,128]{3,1,2,0:T(8,128)S(1)} %bitcast.132), channel_id=1, source_target_pairs={{0,24},{8,16},{16,8},{24,0},{1,25},{9,17},{17,9},{25,1},{2,26},{10... | collective-permute-start | bytes 6291464 | tf_op jit(solution)/shard_map/ppermute | solution.py:28
  44.5 90.7 %collective-permute-start = (f32[32,64,2,128]{3,1,2,0:T(8,128)S(1)}, f32[32,64,2,128]{3,1,2,0:T(8,128)S(1)}, u32[]{:S(2)}, u32[]{:S(2)}) collective-permute-start(f32[32,64,2,128]{3,1,2,0:T(8,128)S(1)} %bitcast.133), channel_id=1, source_target_pairs={{0,8},{8,0},{16,24},{24,16},{1,9},{9,1},{17,25},{25,17},{2,10},{10... | collective-permute-start | bytes 6291464 | tf_op jit(solution)/shard_map/ppermute | solution.py:28
  45.2 90.0 %collective-permute-start.1 = (f32[32,64,2,128]{3,1,2,0:T(8,128)S(1)}, f32[32,64,2,128]{3,1,2,0:T(8,128)S(1)}, u32[]{:S(2)}, u32[]{:S(2)}) collective-permute-start(f32[32,64,2,128]{3,1,2,0:T(8,128)S(1)} %bitcast.134), channel_id=1, source_target_pairs={{0,16},{8,24},{16,0},{24,8},{1,17},{9,25},{17,1},{25,9},{2,18},{10... | collective-permute-start | bytes 6291464 | tf_op jit(solution)/shard_map/ppermute | solution.py:28
  206.4 369.6 %all-to-all-start = ((f32[32,128,2,512]{1,2,0,3:T(2,128)}), f32[32,128,2,512]{1,2,0,3:T(2,128)}, u32[]{:S(2)}, u32[]{:S(2)}) async-start(f32[32,128,2,512]{1,2,0,3:T(2,128)} %copy.31), calls=%async_computation | async-start | bytes 33554432 | tf_op jit(solution)/shard_map/all_to_all | solution.py:74
  586.9 1.8 copy-start.2
  588.7 71.4 %copy-start.3 = (f32[1,512,2,256]{3,1,0,2:T(8,128)S(1)}, f32[1,512,2,256]{3,1,0,2:T(8,128)}, u32[]{:S(2)}) copy-start(f32[1,512,2,256]{3,1,0,2:T(8,128)} %get-tuple-element.10) | copy-start | bytes 3145732
  1121.7 7.0 copy-start.4
  1179.6 97.9 %all-to-all-start.2 = ((f32[128,32,2,256]{0,2,1,3:T(2,128)}), f32[128,32,2,256]{0,2,1,3:T(2,128)}, u32[]{:S(2)}, u32[]{:S(2)}) async-start(f32[128,32,2,256]{0,2,1,3:T(2,128)} %copy.42), calls=%async_computation.2 | async-start | bytes 16777216 | tf_op jit(solution)/shard_map/all_to_all | solution.py:86
  1277.5 16.9 %copy-start.1 = (f32[32,64,256]{2,1,0:T(8,128)S(1)}, f32[32,64,256]{2,1,0:T(8,128)}, u32[]{:S(2)}) copy-start(f32[32,64,256]{2,1,0:T(8,128)} %param.2) | copy-start | bytes 6291460
